TPU v7x, 32 devices: a whole 2x2x4 slice. The times are simulated.
32 devices in a mesh: groups: 2 (over x), elem: 16 (over z, y, core).
Axes of the slice: x: 2, y: 2, z: 4, core: 2. Of those that a mesh axis runs over, the one named last changes fastest.
Arguments:
- snapshots: float32 [2, 4096, 16384], P(None, ('groups', 'elem')), parts along dimension 1, may hold values from -6 to 6
- delays: float32 [384, 2048], replicated, may hold values from -3 to 3
- element_order: int32 [4096], P('groups'), parts along dimension 0, may hold values from 0 to 2047, each once
- beam_table: int32 [512], P('groups'), parts along dimension 0, may hold values from 0 to 383
- band_len: int32 [8], replicated, may hold values from 1 to 4, 16 in all
Outputs:
- beams: float32 [16384, 2, 512], P('elem', None, 'groups'), parts along dimension 2
- power_db: float32 [8, 512], P(None, 'groups'), parts along dimension 1
There are 2 independent parts, one for each index of `groups`. A program takes and returns all parts, laid end to end along the dimension named above; an argument that names none is the same for every part. Nothing has to cross between parts.
Inputs may be any that keep to these rules, and one draw needn't show every extreme that they name: `element_order`: each of 0 to 2047 appears once. `band_len`: the entries sum to 16.
All inputs are finite; a program needn't handle non-finite values.
Results may differ from a plain program's by a relative error of at most 0.0003.
Values sent between devices are 32-bit elements; how exact they have to be, the bound alone decides.
A program may use at most 128 MiB of HBM per device.

v0:
```python
import functools
import math

import jax
import jax.numpy as jnp
from jax import lax
from jax.experimental import pallas as pl
from jax.experimental.pallas import tpu as pltpu
from jax.sharding import PartitionSpec as P

epsilon = 1e-06
SIDE = 2
RING = 4
CHUNKS = 8


def band_of(band_len, position, unit_count):
    band_ends = jnp.cumsum(band_len)
    band_index = jnp.sum((band_ends <= position).astype(jnp.int32))
    selector = jnp.arange(band_len.shape[0], dtype=jnp.int32) == band_index
    band_size = jnp.sum(jnp.where(selector, band_len, 0))
    band_start = jnp.sum(jnp.where(selector, band_ends, 0)) - band_size
    frequency = (band_start.astype(jnp.float32) + 0.5 * band_size.astype(jnp.float32)) / float(
        unit_count
    )
    return (frequency, band_size, selector.astype(jnp.float32))


def sincos(turns):
    reduced = turns - jnp.floor(turns + 0.5)
    x = reduced * math.pi
    q = x * x
    sin_terms = [(-1.0) ** i / math.factorial(2 * i + 1) for i in range(7)]
    cos_terms = [(-1.0) ** i / math.factorial(2 * i) for i in range(8)]
    s = jnp.full_like(q, sin_terms[-1])
    for term in sin_terms[-2::-1]:
        s = s * q + term
    s = s * x
    c = jnp.full_like(q, cos_terms[-1])
    for term in cos_terms[-2::-1]:
        c = c * q + term
    return 2.0 * s * c, 1.0 - 2.0 * s * s


def split2(v):
    high = v.astype(jnp.bfloat16)
    return high, (v - high.astype(jnp.float32)).astype(jnp.bfloat16)


def split3(v):
    high = v.astype(jnp.bfloat16)
    rest = v - high.astype(jnp.float32)
    middle = rest.astype(jnp.bfloat16)
    return high, middle, (rest - middle.astype(jnp.float32)).astype(jnp.bfloat16)


def kernel(
    n, freq, x, delays, order, table, out, power,
    g1, dt, wh, wl, xa, xb, xz, pa, pb, ra, rb, ry2, pw, tot,
    own_a, own_b, sa_s, sa_r, sb_s, sb_r, sy_s, sy_r, sz_s, sz_r,
    a_s, a_r, b_s, b_r, y2_s, y2_r, p_s, p_r,
):
    me = lax.axis_index("elem")
    core = me % SIDE
    y = (me // SIDE) % SIDE
    z = me // (SIDE * SIDE)
    upper = z // 2
    end = z + upper * (RING - 1 - 2 * z)
    unit_cols = x.shape[2] // n
    chunk = unit_cols // CHUNKS
    early = CHUNKS - 1
    early_cols = early * chunk
    beams = table.shape[0]
    scaling = float(delays.shape[1]) ** (-0.5)
    slots = (3, 2, 1 - end, end)

    def chip(u):
        return u + upper * (RING - 1 - 2 * u)

    def dev(zz, yy, cc):
        return (zz * SIDE + yy % SIDE) * SIDE + cc % SIDE

    ahead = dev(chip(end + 1), y, core)
    beside = dev(chip(1 - end), y, core)

    barrier = pltpu.get_barrier_semaphore()

    def greet(k, carry):
        pl.semaphore_signal(barrier, inc=1, device_id={"elem": (me + k) % n},
                            device_id_type=pl.DeviceIdType.MESH)
        return carry

    lax.fori_loop(1, n, greet, 0)
    pl.semaphore_wait(barrier, n - 1)

    def remote(src, dst, send, recv, target):
        return pltpu.make_async_remote_copy(
            src_ref=src, dst_ref=dst, send_sem=send, recv_sem=recv,
            device_id={"elem": target}, device_id_type=pl.DeviceIdType.MESH)

    def cols(unit, start, size):
        return x.at[:, :, pl.ds(pl.multiple_of(unit * unit_cols + start, 128), size)]

    def part(k):
        return pl.ds(pl.multiple_of(k * chunk, 128), chunk)

    def y_copy(j, k, r):
        return remote(
            cols(dev(chip(slots[j]), y + 1, core + r), k * chunk, chunk),
            xa.at[2 + r, j, :, :, part(k)],
            sy_s.at[r, j, k], sy_r.at[r, j, k], dev(z, y + 1, core + r))

    def z_copy(j, yr, r):
        return remote(
            cols(dev(chip(3 - j), y + yr, core + r), early_cols, chunk), xz.at[j, r, yr],
            sz_s.at[j, r, yr], sz_r.at[j, r, yr], dev(chip(1 - end), y, core + r))

    def a_copy(j, k):
        to = j + 3 * end if j < 2 else 2
        return remote(pa.at[j, k], ra.at[to, k], a_s.at[j, k], a_r.at[to, k],
                      ahead if j < 2 else beside)

    def a_wait(to, k):
        remote(pa.at[0, k], ra.at[to, k], a_s.at[0, k], a_r.at[to, k], beside).wait_recv()

    def b_copy(j, yr):
        return remote(pb.at[j, yr], rb.at[j, yr], b_s.at[j, yr], b_r.at[j, yr],
                      ahead if j < 2 else beside)

    everyone = [(yr, j, r) for j in range(3) for yr in (1, 0) for r in (0, 1)]

    @pl.when(end == 0)
    def _():
        for yr, j, r in everyone:
            z_copy(j, yr, r).start()

    for j in range(4):
        def y_start(k, carry, j=j):
            for r in (0, 1):
                y_copy(j, k, r).start()
            return carry

        lax.fori_loop(0, early, y_start, 0)

    ca, cb, la, lb = {}, {}, {}, {}
    for j in range(4):
        there = dev(chip(slots[j]), y, core + 1)
        here = dev(chip(slots[j]), y, core)
        ca[j] = remote(cols(there, 0, early_cols), xa.at[1, j],
                       sa_s.at[j], sa_r.at[j], dev(z, y, core + 1))
        la[j] = pltpu.make_async_copy(cols(here, 0, early_cols), xa.at[0, j], own_a.at[j])
        ca[j].start()
        la[j].start()
        if j > 0:
            continue
        for i in range(4):
            for yr in (1, 0):
                there = dev(chip(slots[i]), y + yr, core + 1)
                here = dev(chip(slots[i]), y + yr, core)
                cb[i, yr] = remote(cols(there, early_cols, chunk), xb.at[1, i, yr],
                                   sb_s.at[i, yr], sb_r.at[i, yr], dev(z, y, core + 1))
                lb[i, yr] = pltpu.make_async_copy(
                    cols(here, early_cols, chunk), xb.at[0, i, yr], own_b.at[i, yr])
                cb[i, yr].start()
                lb[i, yr].start()

    beam_hot = jnp.where(
        lax.broadcasted_iota(jnp.int32, (beams, delays.shape[0]), 1) == table[...], 1.0, 0.0
    ).astype(jnp.bfloat16)
    step = 512 if delays.shape[1] % 512 == 0 else delays.shape[1]

    def pick_beams(i, carry):
        span = pl.ds(pl.multiple_of(i * step, step), step)
        parts = split3(delays[:, span])
        rows = [jnp.dot(beam_hot, piece, preferred_element_type=jnp.float32) for piece in parts]
        for m, piece in enumerate(rows):
            g1[m * beams:(m + 1) * beams, span] = piece.astype(jnp.bfloat16)
        return carry

    lax.fori_loop(0, delays.shape[1] // step, pick_beams, 0)

    def pick_elems(s, carry):
        r, g = s % 2, s // 2
        u = end + (g // 2) * (1 - 2 * end)
        q = dev(chip(u), y + g % 2, core + r)
        row = order[q]
        hot = jnp.where(
            lax.broadcasted_iota(jnp.int32, (delays.shape[1], row.shape[1]), 0) == row, 1.0, 0.0
        ).astype(jnp.bfloat16)
        got = jnp.dot(g1[...], hot, preferred_element_type=jnp.float32)
        dt[s] = got[:beams] + got[beams:2 * beams] + got[2 * beams:]
        return carry

    lax.fori_loop(0, 6, pick_elems, 0)
    wide = 2 * x.shape[1]

    def weigh(f, sources):
        for i, s in enumerate(sources):
            sine, cosine = sincos(f * dt[s])
            ch, cl = split2(cosine * scaling)
            sh, sl = split2(sine * scaling)
            span = slice(i * wide, (i + 1) * wide)
            wh[:beams, span] = jnp.concatenate([ch, sh], axis=1)
            wh[beams:, span] = jnp.concatenate([-sh, ch], axis=1)
            wl[:beams, span] = jnp.concatenate([cl, sl], axis=1)
            wl[beams:, span] = jnp.concatenate([-sl, cl], axis=1)

    def form(pieces):
        rows = jnp.concatenate([piece.reshape(wide, chunk) for piece in pieces], axis=0)
        xh, xl = split2(rows)
        span = slice(0, wide * len(pieces))
        dot = functools.partial(jnp.dot, preferred_element_type=jnp.float32)
        high = wh[:, span]
        return dot(high, xh) + (dot(high, xl) + dot(wl[:, span], xh))

    def a_slot(j, then):
        weigh(freq[dev(chip(slots[j]), y, core)], (0, 1, 2, 3))
        la[j].wait()
        ca[j].wait_recv()

        def one(k, carry):
            for r in (0, 1):
                y_copy(j, k, r).wait_recv()
            pa[j, k] = form([xa[s, j, :, :, part(k)] for s in range(4)])
            then(k)
            return carry

        lax.fori_loop(0, early, one, 0)

    def join(j, to, k):
        a_wait(to, k)
        pa[j, k] += ra[to, k]

    def after0(k):
        @pl.when(end == 0)
        def _():
            a_copy(0, k).start()

    def after1(k):
        @pl.when(end == 0)
        def _():
            a_copy(1, k).start()

        @pl.when(end == 1)
        def _():
            join(0, 0, k)
            a_copy(0, k).start()

    def after2(k):
        @pl.when(end == 1)
        def _():
            join(2, 3, k)

        a_copy(2, k).start()

        @pl.when(end == 1)
        def _():
            join(1, 1, k)
            a_copy(1, k).start()

    def emit(got, start):
        out[pl.ds(pl.multiple_of(start, 128), chunk), :] = got
        tot[...] += jnp.sum(got * got, axis=0, keepdims=True)

    def after3(k):
        @pl.when(end == 1)
        def _():
            join(3, 4, k)

        a_wait(2, k)
        emit((pa[3, k] + ra[2, k]).T, k * chunk)

    tot[...] = jnp.zeros_like(tot)
    a_slot(0, after0)

    for i in range(4):
        for yr in (1, 0):
            lb[i, yr].wait()
            cb[i, yr].wait_recv()

    @pl.when(end == 1)
    def _():
        for yr, j, r in everyone:
            z_copy(j, yr, r).wait_recv()

        def b_joint(t, carry):
            i, yr = t // 2, 1 - t % 2
            j = i + i // 2
            weigh(freq[dev(chip(3 - i), y + yr, core)], (0, 1, 4, 5))
            pb[j, yr] = form([xb[0, j, yr], xb[1, j, yr], xz[i, 0, yr], xz[i, 1, yr]])
            return carry

        lax.fori_loop(0, 6, b_joint, 0)
        for j in (0, 1):
            for yr in (1, 0):
                b_copy(j, yr).start()

    def b_end(t, carry):
        yr = 1 - t
        weigh(freq[dev(chip(0), y + yr, core)], (0, 1))
        pb[3 - end, yr] = form([xb[0, 3 - end, yr], xb[1, 3 - end, yr]])
        return carry

    lax.fori_loop(0, 2, b_end, 0)
    a_slot(1, after1)

    @pl.when(end == 1)
    def _():
        for yr in (1, 0):
            b_copy(0, yr).wait_recv()
            pb[2, yr] += rb[0, yr]
            b_copy(2, yr).start()
        for yr in (1, 0):
            b_copy(1, yr).wait_recv()
            pb[3, yr] += rb[1, yr]

    a_slot(2, after2)

    @pl.when(end == 0)
    def _():
        for yr in (1, 0):
            b_copy(2, yr).wait_recv()
            pb[3, yr] += rb[2, yr]

    last = remote(pb.at[3, 1], ry2, y2_s, y2_r, dev(z, y + 1, core))
    last.start()
    a_slot(3, after3)
    last.wait_recv()
    emit((pb[3, 0] + ry2[...]).T, early_cols)
    both = tot[:, :beams] + tot[:, beams:]
    pw[0] = jnp.broadcast_to(both, pw.shape[1:])

    def p_copy(k):
        return remote(pw.at[0], pw.at[k], p_s.at[k], p_r.at[k], (me + k) % n)

    def p_start(k, carry):
        p_copy(k).start()
        return carry

    def p_wait(k, carry):
        p_copy(k).wait()
        return carry

    lax.fori_loop(1, n, p_start, 0)
    last.wait_send()
    for j in range(4):
        ca[j].wait_send()
        for yr in (1, 0):
            cb[j, yr].wait_send()

        def drain(k, carry, j=j):
            for r in (0, 1):
                y_copy(j, k, r).wait_send()
            if j < 3:
                a_copy(j, k).wait_send()
            return carry

        lax.fori_loop(0, early, drain, 0)

    @pl.when(end == 0)
    def _():
        for yr, j, r in everyone:
            z_copy(j, yr, r).wait_send()

    @pl.when(end == 1)
    def _():
        for j in range(3):
            for yr in (1, 0):
                b_copy(j, yr).wait_send()

    lax.fori_loop(1, n, p_wait, 0)
    power[...] = pw[...]


def local_ring(n, snapshots, delays, element_order, beam_table, band_len):
    local_elems = snapshots.shape[1]
    unit_cols = snapshots.shape[2] // n
    beams = beam_table.shape[0]
    early, chunk = CHUNKS - 1, unit_cols // CHUNKS
    block = (2 * beams, chunk)
    units = jnp.arange(n, dtype=jnp.int32)
    frequency, band_size, selector = jax.vmap(lambda u: band_of(band_len, u, n))(units)
    f32, sem = jnp.float32, pltpu.SemaphoreType.DMA
    raw = (2, local_elems)
    vmem, hbm, smem = (pl.BlockSpec(memory_space=m) for m in (pltpu.VMEM, pl.ANY, pltpu.SMEM))
    formed, power = pl.pallas_call(
        functools.partial(kernel, n),
        out_shape=(
            jax.ShapeDtypeStruct((unit_cols, 2 * beams), f32),
            jax.ShapeDtypeStruct((n, 8, beams), f32),
        ),
        in_specs=[smem, hbm, vmem, vmem, vmem],
        out_specs=(vmem, vmem),
        scratch_shapes=[
            pltpu.VMEM((3 * beams, delays.shape[1]), jnp.bfloat16),
            pltpu.VMEM((6, beams, local_elems), f32),
            pltpu.VMEM((2 * beams, 8 * local_elems), jnp.bfloat16),
            pltpu.VMEM((2 * beams, 8 * local_elems), jnp.bfloat16),
            pltpu.VMEM((4, 4) + raw + (early * chunk,), f32),
            pltpu.VMEM((2, 4, 2) + raw + (chunk,), f32),
            pltpu.VMEM((3, 2, 2) + raw + (chunk,), f32),
            pltpu.VMEM((4, early) + block, f32),
            pltpu.VMEM((4, 2) + block, f32),
            pltpu.VMEM((5, early) + block, f32),
            pltpu.VMEM((3, 2) + block, f32),
            pltpu.VMEM(block, f32),
            pltpu.VMEM((n, 8, beams), f32),
            pltpu.VMEM((1, 2 * beams), f32),
            sem((4,)), sem((4, 2)),
            sem((4,)), sem((4,)), sem((4, 2)), sem((4, 2)),
            sem((2, 4, early)), sem((2, 4, early)), sem((3, 2, 2)), sem((3, 2, 2)),
            sem((3, early)), sem((5, early)), sem((3, 2)), sem((3, 2)),
            sem, sem,
            sem((n,)), sem((n,)),
        ],
        compiler_params=pltpu.CompilerParams(
            collective_id=0, has_side_effects=True, vmem_limit_bytes=62 * 1024 * 1024
        ),
    )(
        frequency, snapshots, delays,
        element_order.reshape(n, 1, local_elems), beam_table.reshape(beams, 1),
    )
    row_unit = (lax.axis_index("elem") + n - units) % n
    share = selector / (band_size.astype(f32) * unit_cols)[:, None]
    summed = jnp.sum(share[row_unit][:, :, None] * power[:, 0][:, None, :], axis=0)
    decibels = 10.0 * jnp.log10(summed + epsilon)
    return (formed.reshape(unit_cols, 2, beams), decibels)


def fits(mesh):
    return mesh.shape["elem"] == SIDE * SIDE * RING


def steering(delays, element_order, beam_table, frequency):
    delay_rows = jnp.take(delays, beam_table, axis=0)
    delay_rows = jnp.take(delay_rows, element_order, axis=1)
    phases = 2.0 * math.pi * frequency * delay_rows
    scaling = float(delays.shape[1]) ** (-0.5)
    cosines = jnp.cos(phases) * scaling
    sines = -jnp.sin(phases) * scaling
    upper_rows = jnp.concatenate([cosines.T, sines.T], axis=1)
    lower_rows = jnp.concatenate([-sines.T, cosines.T], axis=1)
    return jnp.concatenate([upper_rows, lower_rows], axis=0)


def project(arrived, weights):
    columns = arrived.shape[2]
    stacked = arrived.reshape(2 * arrived.shape[1], columns)
    return lax.dot_general(
        stacked,
        weights,
        (((0,), (0,)), ((), ())),
        precision=lax.Precision.HIGHEST,
        preferred_element_type=jnp.float32,
    )


def local(snapshots, delays, element_order, beam_table, band_len):
    unit_count = lax.axis_size("elem")
    position = lax.axis_index("elem")
    frequency, band_size, selector = band_of(band_len, position, unit_count)
    weights = steering(delays, element_order, beam_table, frequency)
    beam_count = beam_table.shape[0]
    local_elems = snapshots.shape[1]
    unit_cols = snapshots.shape[2] // unit_count
    divided = snapshots.reshape(2, local_elems, unit_count, unit_cols)
    pieces = lax.all_to_all(divided, "elem", split_axis=2, concat_axis=1, tiled=True)
    formed = project(pieces.reshape(2, pieces.shape[1], pieces.shape[3]), weights)
    column_count = formed.shape[0]
    squares = jnp.sum(formed * formed, axis=0)
    power_mean = (squares[:beam_count] + squares[beam_count:]) / (
        band_size.astype(jnp.float32) * column_count
    )
    partial_value = selector[:, None] * power_mean[None, :]
    summed = lax.psum(partial_value, "elem")
    decibels = 10.0 * jnp.log10(summed + epsilon)
    return (formed.reshape(column_count, 2, beam_count), decibels)


def solution(mesh):
    n = mesh.shape["elem"]
    body = functools.partial(local_ring, n) if fits(mesh) else local
    return jax.shard_map(
        body,
        mesh=mesh,
        in_specs=(P(None, ("groups", "elem"), None), P(), P("groups"), P("groups"), P()),
        out_specs=(P("elem", None, "groups"), P(None, "groups")),
        check_vma=False,
    )
```

profile of v0, /device:TPU:0, one launch (start us, length us, event | category | flops | bytes accessed | tf_op | source)
XLA Modules:
  0.0 191.1 jit_solution(5903704836650156542)
XLA Ops:
  0.6 0.8 reduce-window.8
  1.5 0.1 convert_reduce_fusion
  1.6 0.8 select_reduce_fusion.1
  2.4 0.5 convert_multiply_fusion
  2.9 0.1 convert_divide_fusion
  3.0 0.6 gather_fusion
  3.6 1.5 copy.8.table
  5.1 180.9 %shard_map.68 = (f32[1024,512]{1,0:T(8,128)}, f32[16,8,256]{2,1,0:T(8,128)}) custom-call(f32[16]{0:T(128)} %get-tuple-element.9.freq, f32[2,128,16384]{2,1,0:T(8,128)} %x.1, f32[384,2048]{1,0:T(8,128)} %delays.1, s32[16,1,128]{2,1,0:T(1,128)} %bitcast.10, s32[256,1]{1,0:T(8,128)} %copy.8.table), custom_call_target="tpu_custom_call" | custom-call | tf_op jit(solution)/shard_map/pallas_call | solution.py:386
  186.0 0.9 slice.3
  186.9 0.1 multiply_reduce_fusion
  187.0 0.6 log_multiply_fusion
  187.6 3.5 %reshape.95 = f32[1024,2,256]{2,1,0:T(2,128)} reshape(f32[1024,512]{1,0:T(8,128)} %get-tuple-element.4) | data formatting | bytes 4194304 | tf_op jit(solution)/shard_map/reshape | solution.py:427
  (3 shorter events, 0.0 us)
where the time goes:
time: 191 us
  Pallas kernels  181 us (95%)
  local copies, waits for them, and re-layouts  6.47 us (3%)
  other arithmetic  3.1 us (2%)
    pallas_call x1, Pallas kernels, local_ring(): pl.pallas_call(functools.partial(kernel, n), out_shape=(jax.ShapeDtypeStr...  181 us

commit v1 on v0

v1 whole, which is shorter than its diff:
```python
import functools
import math

import jax
import jax.numpy as jnp
from jax import lax
from jax.experimental import pallas as pl
from jax.experimental.pallas import tpu as pltpu
from jax.sharding import PartitionSpec as P

epsilon = 1e-06
SIDE = 2
RING = 4
CHUNKS = 8


def band_of(band_len, position, unit_count):
    band_ends = jnp.cumsum(band_len)
    band_index = jnp.sum((band_ends <= position).astype(jnp.int32))
    selector = jnp.arange(band_len.shape[0], dtype=jnp.int32) == band_index
    band_size = jnp.sum(jnp.where(selector, band_len, 0))
    band_start = jnp.sum(jnp.where(selector, band_ends, 0)) - band_size
    frequency = (band_start.astype(jnp.float32) + 0.5 * band_size.astype(jnp.float32)) / float(
        unit_count
    )
    return (frequency, band_size, selector.astype(jnp.float32))


def sincos(turns):
    reduced = turns - jnp.floor(turns + 0.5)
    x = reduced * math.pi
    q = x * x
    sin_terms = [(-1.0) ** i / math.factorial(2 * i + 1) for i in range(7)]
    cos_terms = [(-1.0) ** i / math.factorial(2 * i) for i in range(8)]
    s = jnp.full_like(q, sin_terms[-1])
    for term in sin_terms[-2::-1]:
        s = s * q + term
    s = s * x
    c = jnp.full_like(q, cos_terms[-1])
    for term in cos_terms[-2::-1]:
        c = c * q + term
    return 2.0 * s * c, 1.0 - 2.0 * s * s


def split2(v):
    high = v.astype(jnp.bfloat16)
    return high, (v - high.astype(jnp.float32)).astype(jnp.bfloat16)


def split3(v):
    high = v.astype(jnp.bfloat16)
    rest = v - high.astype(jnp.float32)
    middle = rest.astype(jnp.bfloat16)
    return high, middle, (rest - middle.astype(jnp.float32)).astype(jnp.bfloat16)


def item_unit(i):
    return 3 - i + (i + RING) // (RING + 1) + i // (RING + 1)


def item_chunk(i):
    return CHUNKS - 2 + (i + RING) // (RING + 1) - i // (RING + 1)


def kernel(
    n, lens, x, delays, order, table, out, power,
    bl, dl, od, tb, g1, dt, wh, wl, xa, xb, xz, pa, pb, ra, rb, ry, pw, tot,
    in_s, own_a, own_b, sa_s, sa_r, sb_s, sb_r, sy_s, sy_r, sz_s, sz_r,
    a_s, a_r, b_s, b_r, y2_s, y2_r, p_s, p_r,
):
    me = lax.axis_index("elem")
    core = me % SIDE
    y = (me // SIDE) % SIDE
    z = me // (SIDE * SIDE)
    upper = z // 2
    end = z + upper * (RING - 1 - 2 * z)
    unit_cols = x.shape[2] // n
    chunk = unit_cols // CHUNKS
    most = CHUNKS - 1
    beams = table.shape[1]
    scaling = float(delays.shape[1]) ** (-0.5)
    slots = (3, 2, 1 - end, end)
    early = (most - 1, most, most - end, most - 1 + end)

    def chip(u):
        return u + upper * (RING - 1 - 2 * u)

    def dev(zz, yy, cc):
        return (zz * SIDE + yy % SIDE) * SIDE + cc % SIDE

    ahead = dev(chip(end + 1), y, core)
    beside = dev(chip(1 - end), y, core)

    barrier = pltpu.get_barrier_semaphore()

    def greet(target):
        pl.semaphore_signal(barrier, inc=1, device_id={"elem": target},
                            device_id_type=pl.DeviceIdType.MESH)

    for r in (0, 1):
        greet(dev(z, y + 1, core + r))
        greet(dev(chip(1 - end), y, core + r))
    greet(dev(z, y, core + 1))

    @pl.when(end == 1)
    def _():
        greet(ahead)

    fetches = [
        pltpu.make_async_copy(lens, bl, in_s.at[0]),
        pltpu.make_async_copy(delays, dl, in_s.at[1]),
        pltpu.make_async_copy(order, od, in_s.at[2]),
        pltpu.make_async_copy(table, tb, in_s.at[3]),
    ]
    for fetch in fetches:
        fetch.start()
    pl.semaphore_wait(barrier, 5 + end)

    def remote(src, dst, send, recv, target):
        return pltpu.make_async_remote_copy(
            src_ref=src, dst_ref=dst, send_sem=send, recv_sem=recv,
            device_id={"elem": target}, device_id_type=pl.DeviceIdType.MESH)

    def cols(unit, start, size):
        return x.at[:, :, pl.ds(pl.multiple_of(unit * unit_cols + start, 128), size)]

    def part(k):
        return pl.ds(pl.multiple_of(k * chunk, 128), chunk)

    def y_copy(j, k, r):
        return remote(
            cols(dev(chip(slots[j]), y + 1, core + r), k * chunk, chunk),
            xa.at[2 + r, j, :, :, part(k)],
            sy_s.at[r, j, k], sy_r.at[r, j, k], dev(z, y + 1, core + r))

    def late(i, yy, cc):
        return cols(dev(chip(item_unit(i)), yy, cc), item_chunk(i) * chunk, chunk)

    def z_copy(i, yr, r):
        return remote(
            late(i, y + yr, core + r), xz.at[i, r, yr],
            sz_s.at[i, r, yr], sz_r.at[i, r, yr], dev(chip(1 - end), y, core + r))

    def b_peer(i, yr):
        return remote(late(i, y + yr, core + 1), xb.at[1, i, yr],
                      sb_s.at[i, yr], sb_r.at[i, yr], dev(z, y, core + 1))

    def b_own(i, yr):
        return pltpu.make_async_copy(late(i, y + yr, core), xb.at[0, i, yr], own_b.at[i, yr])

    def a_copy(j, k):
        to = j + 3 * end if j < 2 else 2
        return remote(pa.at[j, k], ra.at[to, k], a_s.at[j, k], a_r.at[to, k],
                      ahead if j < 2 else beside)

    def a_wait(to, k):
        remote(pa.at[0, k], ra.at[to, k], a_s.at[0, k], a_r.at[to, k], beside).wait_recv()

    def b_copy(i, yr):
        to = i if i < 3 else i - 1
        return remote(pb.at[i, yr], rb.at[to, yr], b_s.at[to, yr], b_r.at[to, yr],
                      ahead if i < 3 else beside)

    def last(i):
        return remote(pb.at[i, 1], ry.at[i - 3], y2_s.at[i - 3], y2_r.at[i - 3],
                      dev(z, y + 1, core))

    def every(low, high, step):
        def body(t, carry):
            step(t)
            return carry

        lax.fori_loop(low, high, body, 0)

    pairs = [(yr, r) for yr in (1, 0) for r in (0, 1)]

    @pl.when(end == 0)
    def _():
        def start(i):
            for yr, r in pairs:
                z_copy(i, yr, r).start()

        every(0, 4, start)

    for j in range(4):
        def y_start(k, j=j):
            for r in (0, 1):
                y_copy(j, k, r).start()

        every(0, early[j], y_start)

    ca, la = {}, {}

    def b_start(i):
        for yr in (1, 0):
            b_peer(i, yr).start()
            b_own(i, yr).start()

    for j in range(4):
        there = dev(chip(slots[j]), y, core + 1)
        here = dev(chip(slots[j]), y, core)
        ca[j] = remote(cols(there, 0, most * chunk), xa.at[1, j],
                       sa_s.at[j], sa_r.at[j], dev(z, y, core + 1))
        la[j] = pltpu.make_async_copy(cols(here, 0, most * chunk), xa.at[0, j], own_a.at[j])
        ca[j].start()
        la[j].start()
        if j == 0:
            every(4 - 4 * end, 6, b_start)

    for fetch in fetches:
        fetch.wait()

    def frequency(unit):
        total, value = 0, 0.0
        for b in range(lens.shape[0]):
            size = bl[b]
            inside = jnp.logical_and(unit >= total, unit < total + size)
            middle = (2 * total + size).astype(jnp.float32) * (0.5 / n)
            value = jnp.where(inside, middle, value)
            total = total + size
        return value

    beam_hot = jnp.where(
        lax.broadcasted_iota(jnp.int32, (delays.shape[0], beams), 0) == tb[...], 1.0, 0.0
    ).T.astype(jnp.bfloat16)
    step = 512 if delays.shape[1] % 512 == 0 else delays.shape[1]

    def pick_beams(i):
        span = pl.ds(pl.multiple_of(i * step, step), step)
        parts = split3(dl[:, span])
        rows = [jnp.dot(beam_hot, piece, preferred_element_type=jnp.float32) for piece in parts]
        for m, piece in enumerate(rows):
            g1[m * beams:(m + 1) * beams, span] = piece.astype(jnp.bfloat16)

    every(0, delays.shape[1] // step, pick_beams)

    def pick_elems(s):
        r, g = s % 2, s // 2
        u = end + (g // 2) * (1 - 2 * end)
        q = dev(chip(u), y + g % 2, core + r)
        row = od[q]
        hot = jnp.where(
            lax.broadcasted_iota(jnp.int32, (delays.shape[1], row.shape[1]), 0) == row, 1.0, 0.0
        ).astype(jnp.bfloat16)
        got = jnp.dot(g1[...], hot, preferred_element_type=jnp.float32)
        dt[s] = got[:beams] + got[beams:2 * beams] + got[2 * beams:]

    every(0, 6, pick_elems)
    wide = 2 * x.shape[1]

    def weigh(f, sources):
        for i, s in enumerate(sources):
            sine, cosine = sincos(f * dt[s])
            ch, cl = split2(cosine * scaling)
            sh, sl = split2(sine * scaling)
            span = slice(i * wide, (i + 1) * wide)
            wh[:beams, span] = jnp.concatenate([ch, sh], axis=1)
            wh[beams:, span] = jnp.concatenate([-sh, ch], axis=1)
            wl[:beams, span] = jnp.concatenate([cl, sl], axis=1)
            wl[beams:, span] = jnp.concatenate([-sl, cl], axis=1)

    def form(pieces):
        rows = jnp.concatenate([piece.reshape(wide, chunk) for piece in pieces], axis=0)
        xh, xl = split2(rows)
        span = slice(0, wide * len(pieces))
        dot = functools.partial(jnp.dot, preferred_element_type=jnp.float32)
        high = wh[:, span]
        return dot(high, xh) + (dot(high, xl) + dot(wl[:, span], xh))

    def a_slot(j, then):
        weigh(frequency(dev(chip(slots[j]), y, core)), (0, 1, 2, 3))
        la[j].wait()
        ca[j].wait_recv()

        def one(k):
            for r in (0, 1):
                y_copy(j, k, r).wait_recv()
            pa[j, k] = form([xa[s, j, :, :, part(k)] for s in range(4)])
            then(k)

        every(0, early[j], one)

    def join(j, to, k):
        a_wait(to, k)
        pa[j, k] += ra[to, k]

    def after0(k):
        @pl.when(end == 0)
        def _():
            a_copy(0, k).start()

    def join0(k):
        join(0, 0, k)
        a_copy(0, k).start()

    def join1(k):
        join(1, 1, k)
        a_copy(1, k).start()

    def after1(k):
        @pl.when(end == 0)
        def _():
            a_copy(1, k).start()

        @pl.when(jnp.logical_and(end == 1, k < early[0]))
        def _():
            join0(k)

    def after2(k):
        @pl.when(end == 1)
        def _():
            join(2, 3, k)

        a_copy(2, k).start()

        @pl.when(end == 1)
        def _():
            join1(k)

    def emit(got, start):
        rows = pl.ds(pl.multiple_of(start, 128), chunk)
        out[rows, 0, :] = got[:, :beams]
        out[rows, 1, :] = got[:, beams:]
        tot[...] += jnp.sum(got * got, axis=0, keepdims=True)

    def after3(k):
        @pl.when(end == 1)
        def _():
            join(3, 4, k)

        a_wait(2, k)
        emit((pa[3, k] + ra[2, k]).T, k * chunk)

    tot[...] = jnp.zeros_like(tot)
    a_slot(0, after0)

    def b_landed(i):
        for yr in (1, 0):
            b_own(i, yr).wait()
            b_peer(i, yr).wait_recv()

    every(4 - 4 * end, 6, b_landed)

    @pl.when(end == 1)
    def _():
        def z_landed(i):
            for yr, r in pairs:
                z_copy(i, yr, r).wait_recv()

        every(0, 4, z_landed)

        def b_joint(t):
            i, yr = t // 2, 1 - t % 2
            weigh(frequency(dev(chip(item_unit(i)), y + yr, core)), (0, 1, 4, 5))
            pb[i, yr] = form([xb[0, i, yr], xb[1, i, yr], xz[i, 0, yr], xz[i, 1, yr]])

        every(0, 8, b_joint)
        for i in range(3):
            for yr in (1, 0):
                b_copy(i, yr).start()

    def b_end(t):
        i, yr = 4 + t % 2, 1 - t // 2
        weigh(frequency(dev(chip(0), y + yr, core)), (0, 1))
        pb[i, yr] = form([xb[0, i, yr], xb[1, i, yr]])

    every(0, 4, b_end)
    a_slot(1, after1)

    @pl.when(end == 1)
    def _():
        for i in range(2):
            for yr in (1, 0):
                b_copy(i, yr).wait_recv()
                pb[5 - i, yr] += rb[i, yr]
                b_copy(5 - i, yr).start()
        for yr in (1, 0):
            b_copy(2, yr).wait_recv()
            pb[3, yr] += rb[2, yr]

    a_slot(2, after2)

    @pl.when(end == 1)
    def _():
        join1(most - 1)
        last(3).start()

    @pl.when(end == 0)
    def _():
        for i in (4, 5):
            for yr in (1, 0):
                b_copy(i, yr).wait_recv()
                pb[i, yr] += rb[i - 1, yr]
            last(i).start()

    a_slot(3, after3)

    def finish(i):
        last(i).wait_recv()
        emit((pb[i, 0] + ry[i - 3]).T, item_chunk(i) * chunk)

    every(4 - end, 6 - 2 * end, finish)
    pw[me] = tot[:, :beams] + tot[:, beams:]

    def p_copy(k):
        return remote(pw.at[me], pw.at[me], p_s.at[k], p_r.at[k], (me + k) % n)

    every(1, n, lambda k: p_copy(k).start())

    def last_sent(i):
        last(i).wait_send()

    every(4 - end, 6 - 2 * end, last_sent)

    def b_sent(i):
        for yr in (1, 0):
            b_peer(i, yr).wait_send()

    every(4 - 4 * end, 6, b_sent)
    for j in range(4):
        ca[j].wait_send()

        def drain(k, j=j):
            for r in (0, 1):
                y_copy(j, k, r).wait_send()
            if j < 3:
                a_copy(j, k).wait_send()

        every(0, early[j], drain)

    @pl.when(end == 0)
    def _():
        def z_sent(i):
            for yr, r in pairs:
                z_copy(i, yr, r).wait_send()

        every(0, 4, z_sent)

    @pl.when(end == 1)
    def _():
        for i in (0, 1, 2, 4, 5):
            for yr in (1, 0):
                b_copy(i, yr).wait_send()

    def p_landed(k):
        p_copy(k).wait_send()
        other = (me + n - k) % n
        remote(pw.at[other], pw.at[other], p_s.at[k], p_r.at[k], other).wait_recv()

    every(1, n, p_landed)
    power[...] = pw[...]


def conclude(n, lens, formed, power, beams, decibels, sems):
    pieces = sems.shape[0]
    rows = formed.shape[0] // pieces
    copies = []
    for i in range(pieces):
        span = pl.ds(i * rows, rows)
        copies.append(pltpu.make_async_copy(formed.at[span], beams.at[span], sems.at[i]))
        copies[-1].start()
    bands = decibels.shape[0]
    band = lax.broadcasted_iota(jnp.int32, decibels.shape, 0)
    low = jnp.zeros(decibels.shape, jnp.int32)
    size = jnp.zeros(decibels.shape, jnp.int32)
    total = 0
    for b in range(bands):
        low = jnp.where(band == b, total, low)
        size = jnp.where(band == b, lens[b], size)
        total = total + lens[b]
    high = low + size
    summed = jnp.zeros(decibels.shape, jnp.float32)
    for u in range(n):
        inside = jnp.logical_and(low <= u, u < high)
        summed = summed + jnp.where(inside, power[u], 0.0)
    mean = summed / (size.astype(jnp.float32) * formed.shape[0])
    decibels[...] = (10.0 / math.log(10.0)) * jnp.log(mean + epsilon)
    for copy in copies:
        copy.wait()


def local_ring(n, snapshots, delays, element_order, beam_table, band_len):
    local_elems = snapshots.shape[1]
    unit_cols = snapshots.shape[2] // n
    beams = beam_table.shape[0]
    most, chunk = CHUNKS - 1, unit_cols // CHUNKS
    block = (2 * beams, chunk)
    f32, sem = jnp.float32, pltpu.SemaphoreType.DMA
    raw = (2, local_elems)
    vmem, hbm, smem = (pl.BlockSpec(memory_space=m) for m in (pltpu.VMEM, pl.ANY, pltpu.SMEM))
    formed, power = pl.pallas_call(
        functools.partial(kernel, n),
        out_shape=(
            pltpu.VMEM((unit_cols, 2, beams), f32),
            pltpu.VMEM((n, 1, beams), f32),
        ),
        in_specs=[hbm] * 5,
        out_specs=(vmem, vmem),
        scratch_shapes=[
            pltpu.SMEM(band_len.shape, jnp.int32),
            pltpu.VMEM(delays.shape, f32),
            pltpu.VMEM((n, 1, local_elems), jnp.int32),
            pltpu.VMEM((1, beams), jnp.int32),
            pltpu.VMEM((3 * beams, delays.shape[1]), jnp.bfloat16),
            pltpu.VMEM((6, beams, local_elems), f32),
            pltpu.VMEM((2 * beams, 8 * local_elems), jnp.bfloat16),
            pltpu.VMEM((2 * beams, 8 * local_elems), jnp.bfloat16),
            pltpu.VMEM((4, 4) + raw + (most * chunk,), f32),
            pltpu.VMEM((2, 6, 2) + raw + (chunk,), f32),
            pltpu.VMEM((4, 2, 2) + raw + (chunk,), f32),
            pltpu.VMEM((4, most) + block, f32),
            pltpu.VMEM((6, 2) + block, f32),
            pltpu.VMEM((5, most) + block, f32),
            pltpu.VMEM((5, 2) + block, f32),
            pltpu.VMEM((3,) + block, f32),
            pltpu.VMEM((n, 1, beams), f32),
            pltpu.VMEM((1, 2 * beams), f32),
            sem((4,)), sem((4,)), sem((6, 2)),
            sem((4,)), sem((4,)), sem((6, 2)), sem((6, 2)),
            sem((2, 4, most)), sem((2, 4, most)), sem((4, 2, 2)), sem((4, 2, 2)),
            sem((3, most)), sem((5, most)), sem((5, 2)), sem((5, 2)),
            sem((3,)), sem((3,)),
            sem((n,)), sem((n,)),
        ],
        compiler_params=pltpu.CompilerParams(
            collective_id=0, has_side_effects=True, vmem_limit_bytes=54 * 1024 * 1024
        ),
    )(
        band_len, snapshots, delays,
        element_order.reshape(n, 1, local_elems), beam_table.reshape(1, beams),
    )
    formed = pltpu.with_memory_space_constraint(formed, pltpu.VMEM)
    power = pltpu.with_memory_space_constraint(power, pltpu.VMEM)
    return pl.pallas_call(
        functools.partial(conclude, n),
        out_shape=(
            jax.ShapeDtypeStruct((unit_cols, 2, beams), f32),
            jax.ShapeDtypeStruct((band_len.shape[0], beams), f32),
        ),
        in_specs=[smem, vmem, vmem],
        out_specs=(hbm, vmem),
        scratch_shapes=[sem((8,))],
    )(band_len, formed, power)


def fits(mesh):
    return mesh.shape["elem"] == SIDE * SIDE * RING


def steering(delays, element_order, beam_table, frequency):
    delay_rows = jnp.take(delays, beam_table, axis=0)
    delay_rows = jnp.take(delay_rows, element_order, axis=1)
    phases = 2.0 * math.pi * frequency * delay_rows
    scaling = float(delays.shape[1]) ** (-0.5)
    cosines = jnp.cos(phases) * scaling
    sines = -jnp.sin(phases) * scaling
    upper_rows = jnp.concatenate([cosines.T, sines.T], axis=1)
    lower_rows = jnp.concatenate([-sines.T, cosines.T], axis=1)
    return jnp.concatenate([upper_rows, lower_rows], axis=0)


def project(arrived, weights):
    columns = arrived.shape[2]
    stacked = arrived.reshape(2 * arrived.shape[1], columns)
    return lax.dot_general(
        stacked,
        weights,
        (((0,), (0,)), ((), ())),
        precision=lax.Precision.HIGHEST,
        preferred_element_type=jnp.float32,
    )


def local(snapshots, delays, element_order, beam_table, band_len):
    unit_count = lax.axis_size("elem")
    position = lax.axis_index("elem")
    frequency, band_size, selector = band_of(band_len, position, unit_count)
    weights = steering(delays, element_order, beam_table, frequency)
    beam_count = beam_table.shape[0]
    local_elems = snapshots.shape[1]
    unit_cols = snapshots.shape[2] // unit_count
    divided = snapshots.reshape(2, local_elems, unit_count, unit_cols)
    pieces = lax.all_to_all(divided, "elem", split_axis=2, concat_axis=1, tiled=True)
    formed = project(pieces.reshape(2, pieces.shape[1], pieces.shape[3]), weights)
    column_count = formed.shape[0]
    squares = jnp.sum(formed * formed, axis=0)
    power_mean = (squares[:beam_count] + squares[beam_count:]) / (
        band_size.astype(jnp.float32) * column_count
    )
    partial_value = selector[:, None] * power_mean[None, :]
    summed = lax.psum(partial_value, "elem")
    decibels = 10.0 * jnp.log10(summed + epsilon)
    return (formed.reshape(column_count, 2, beam_count), decibels)


def solution(mesh):
    n = mesh.shape["elem"]
    body = functools.partial(local_ring, n) if fits(mesh) else local
    return jax.shard_map(
        body,
        mesh=mesh,
        in_specs=(P(None, ("groups", "elem"), None), P(), P("groups"), P("groups"), P()),
        out_specs=(P("elem", None, "groups"), P(None, "groups")),
        check_vma=False,
    )
```

time: 191 us -> 183 us (0.958)
  local copies, waits for them, and re-layouts: 6.47 us -> 0 us
  other arithmetic: 3.1 us -> 0 us
    reshape x2 -> x0, local copies, waits for them, and re-layouts: 4.99 us -> none  [the longest x1 3.51 us: local_ring(): return (formed.reshape(unit_cols, 2, beams), decibels)]
    pallas_call x1 -> x2, Pallas kernels: 181 us -> 182 us  [the longest x1 180 us: local_ring(): pl.pallas_call(functools.partial(kernel, n), out_shape=(pltpu.VMEM((unit_...]
where the time goes in v1:
time: 183 us
  Pallas kernels  182 us (99%)
    pallas_call x1, Pallas kernels, local_ring(): pl.pallas_call(functools.partial(kernel, n), out_shape=(pltpu.VMEM((unit_...  180 us

profile of v1, /device:TPU:0, one launch (start us, length us, event | category | flops | bytes accessed | tf_op | source)
XLA Modules:
  0.0 183.1 jit_solution(13873455042320434711)
XLA Ops:
  0.6 179.8 %shard_map.68 = (f32[1024,2,256]{2,1,0:T(2,128)S(1)}, f32[16,1,256]{2,1,0:T(1,128)S(1)}) custom-call(s32[8]{0:T(128)} %lens.3, f32[2,128,16384]{2,1,0:T(8,128)} %x.1, f32[384,2048]{1,0:T(8,128)} %delays.1, s32[16,1,128]{2,1,0:T(1,128)} %bitcast.2, s32[1,256]{1,0:T(1,128)} %bitcast.3), custom_call_target="tpu_custom_call" | custom-call | tf_op jit(solution)/shard_map/pallas_call | solution.py:491
  180.4 2.6 %shard_map.69 = (f32[1024,2,256]{2,1,0:T(2,128)}, f32[8,256]{1,0:T(8,128)}) custom-call(s32[8]{0:T(128)} %lens.3, f32[1024,2,256]{2,1,0:T(2,128)S(1)} %get-tuple-element.4.formed, f32[16,1,256]{2,1,0:T(1,128)S(1)} %get-tuple-element.5.power), custom_call_target="tpu_custom_call" | custom-call | tf_op jit(solution)/shard_map/pallas_call | solution.py:534

commit v2 on v1

--- a/solution.py
+++ b/solution.py
@@ -156,10 +156,12 @@
     def a_wait(to, k):
         remote(pa.at[0, k], ra.at[to, k], a_s.at[0, k], a_r.at[to, k], beside).wait_recv()
 
-    def b_copy(i, yr):
-        to = i if i < 3 else i - 1
-        return remote(pb.at[i, yr], rb.at[to, yr], b_s.at[to, yr], b_r.at[to, yr],
-                      ahead if i < 3 else beside)
+    def b_ahead(i, yr):
+        return remote(pb.at[i, yr], rb.at[i, yr], b_s.at[i, yr], b_r.at[i, yr], ahead)
+
+    def b_back(i, yr):
+        return remote(pb.at[i, yr], rb.at[i - 1, yr], b_s.at[i - 1, yr], b_r.at[i - 1, yr],
+                      beside)
 
     def last(i):
         return remote(pb.at[i, 1], ry.at[i - 3], y2_s.at[i - 3], y2_r.at[i - 3],
@@ -332,35 +334,32 @@
         emit((pa[3, k] + ra[2, k]).T, k * chunk)
 
     tot[...] = jnp.zeros_like(tot)
+
+    def b_landed(i, yr):
+        b_own(i, yr).wait()
+        b_peer(i, yr).wait_recv()
+
+    def b_joint(i, yr):
+        for r in (0, 1):
+            z_copy(i, yr, r).wait_recv()
+        b_landed(i, yr)
+        weigh(frequency(dev(chip(item_unit(i)), y + yr, core)), (0, 1, 4, 5))
+        pb[i, yr] = form([xb[0, i, yr], xb[1, i, yr], xz[i, 0, yr], xz[i, 1, yr]])
+
+    @pl.when(end == 1)
+    def _():
+        def b_first(t):
+            i, yr = t // 2, 1 - t % 2
+            b_joint(i, yr)
+            b_ahead(i, yr).start()
+
+        every(0, 6, b_first)
+
     a_slot(0, after0)
-
-    def b_landed(i):
-        for yr in (1, 0):
-            b_own(i, yr).wait()
-            b_peer(i, yr).wait_recv()
-
-    every(4 - 4 * end, 6, b_landed)
-
-    @pl.when(end == 1)
-    def _():
-        def z_landed(i):
-            for yr, r in pairs:
-                z_copy(i, yr, r).wait_recv()
-
-        every(0, 4, z_landed)
-
-        def b_joint(t):
-            i, yr = t // 2, 1 - t % 2
-            weigh(frequency(dev(chip(item_unit(i)), y + yr, core)), (0, 1, 4, 5))
-            pb[i, yr] = form([xb[0, i, yr], xb[1, i, yr], xz[i, 0, yr], xz[i, 1, yr]])
-
-        every(0, 8, b_joint)
-        for i in range(3):
-            for yr in (1, 0):
-                b_copy(i, yr).start()
 
     def b_end(t):
         i, yr = 4 + t % 2, 1 - t // 2
+        b_landed(i, yr)
         weigh(frequency(dev(chip(0), y + yr, core)), (0, 1))
         pb[i, yr] = form([xb[0, i, yr], xb[1, i, yr]])
 
@@ -371,12 +370,17 @@
     def _():
         for i in range(2):
             for yr in (1, 0):
-                b_copy(i, yr).wait_recv()
+                b_ahead(i, yr).wait_recv()
                 pb[5 - i, yr] += rb[i, yr]
-                b_copy(5 - i, yr).start()
-        for yr in (1, 0):
-            b_copy(2, yr).wait_recv()
+                b_back(5 - i, yr).start()
+
+        def b_home(t):
+            yr = 1 - t
+            b_joint(3, yr)
+            b_ahead(2, yr).wait_recv()
             pb[3, yr] += rb[2, yr]
+
+        every(0, 2, b_home)
 
     a_slot(2, after2)
 
@@ -389,7 +393,7 @@
     def _():
         for i in (4, 5):
             for yr in (1, 0):
-                b_copy(i, yr).wait_recv()
+                b_back(i, yr).wait_recv()
                 pb[i, yr] += rb[i - 1, yr]
             last(i).start()
 
@@ -438,9 +442,11 @@
 
     @pl.when(end == 1)
     def _():
-        for i in (0, 1, 2, 4, 5):
-            for yr in (1, 0):
-                b_copy(i, yr).wait_send()
+        for yr in (1, 0):
+            for i in range(3):
+                b_ahead(i, yr).wait_send()
+            for i in (4, 5):
+                b_back(i, yr).wait_send()
 
     def p_landed(k):
         p_copy(k).wait_send()

time: 183 us -> 175 us (0.956)
  Pallas kernels: 182 us -> 174 us
    pallas_call x1, Pallas kernels: 180 us -> 171 us  [local_ring(): pl.pallas_call(functools.partial(kernel, n), out_shape=(pltpu.VMEM((unit_...]
where the time goes in v2:
time: 175 us
  Pallas kernels  174 us (99%)
    pallas_call x1, Pallas kernels, local_ring(): pl.pallas_call(functools.partial(kernel, n), out_shape=(pltpu.VMEM((unit_...  171 us

profile of v2, /device:TPU:0, one launch (start us, length us, event | category | flops | bytes accessed | tf_op | source)
XLA Modules:
  0.0 174.7 jit_solution(1307885352715795073)
XLA Ops:
  0.6 171.2 %shard_map.68 = (f32[1024,2,256]{2,1,0:T(2,128)S(1)}, f32[16,1,256]{2,1,0:T(1,128)S(1)}) custom-call(s32[8]{0:T(128)} %lens.3, f32[2,128,16384]{2,1,0:T(8,128)} %x.1, f32[384,2048]{1,0:T(8,128)} %delays.1, s32[16,1,128]{2,1,0:T(1,128)} %bitcast.2, s32[1,256]{1,0:T(1,128)} %bitcast.3), custom_call_target="tpu_custom_call" | custom-call | tf_op jit(solution)/shard_map/pallas_call | solution.py:497
  171.9 2.6 %shard_map.69 = (f32[1024,2,256]{2,1,0:T(2,128)}, f32[8,256]{1,0:T(8,128)}) custom-call(s32[8]{0:T(128)} %lens.3, f32[1024,2,256]{2,1,0:T(2,128)S(1)} %get-tuple-element.4.formed, f32[16,1,256]{2,1,0:T(1,128)S(1)} %get-tuple-element.5.power), custom_call_target="tpu_custom_call" | custom-call | tf_op jit(solution)/shard_map/pallas_call | solution.py:540

commit v3 on v2

--- a/solution.py
+++ b/solution.py
@@ -63,7 +63,7 @@
 
 
 def kernel(
-    n, lens, x, delays, order, table, out, power,
+    n, lens, x, delays, order, table, out, power, bands,
     bl, dl, od, tb, g1, dt, wh, wl, xa, xb, xz, pa, pb, ra, rb, ry, pw, tot,
     in_s, own_a, own_b, sa_s, sa_r, sb_s, sb_r, sy_s, sy_r, sz_s, sz_r,
     a_s, a_r, b_s, b_r, y2_s, y2_r, p_s, p_r,
@@ -176,20 +176,30 @@
 
     pairs = [(yr, r) for yr in (1, 0) for r in (0, 1)]
 
-    @pl.when(end == 0)
-    def _():
-        def start(i):
-            for yr, r in pairs:
-                z_copy(i, yr, r).start()
-
-        every(0, 4, start)
-
-    for j in range(4):
-        def y_start(k, j=j):
+    def y_start(j):
+        def start(k):
             for r in (0, 1):
                 y_copy(j, k, r).start()
 
-        every(0, early[j], y_start)
+        every(0, early[j], start)
+
+    @pl.when(end == 0)
+    def _():
+        for r in (0, 1):
+            z_copy(0, 1, r).start()
+
+    y_start(0)
+
+    @pl.when(end == 0)
+    def _():
+        def start(t):
+            for r in (0, 1):
+                z_copy(t // 2, 1 - t % 2, r).start()
+
+        every(1, 8, start)
+
+    for j in (1, 2, 3):
+        y_start(j)
 
     ca, la = {}, {}
 
@@ -222,6 +232,13 @@
             total = total + size
         return value
 
+    band = lax.broadcasted_iota(jnp.int32, bands.shape[1:], 0)
+    total = 0
+    for b in range(lens.shape[0]):
+        bands[0] = jnp.where(band == b, total, bands[0] if b else 0)
+        bands[1] = jnp.where(band == b, bl[b], bands[1] if b else 0)
+        total = total + bl[b]
+
     beam_hot = jnp.where(
         lax.broadcasted_iota(jnp.int32, (delays.shape[0], beams), 0) == tb[...], 1.0, 0.0
     ).T.astype(jnp.bfloat16)
@@ -269,7 +286,7 @@
         high = wh[:, span]
         return dot(high, xh) + (dot(high, xl) + dot(wl[:, span], xh))
 
-    def a_slot(j, then):
+    def a_slot(j, then, pause=None):
         weigh(frequency(dev(chip(slots[j]), y, core)), (0, 1, 2, 3))
         la[j].wait()
         ca[j].wait_recv()
@@ -280,7 +297,12 @@
             pa[j, k] = form([xa[s, j, :, :, part(k)] for s in range(4)])
             then(k)
 
-        every(0, early[j], one)
+        if pause is None:
+            every(0, early[j], one)
+        else:
+            every(0, early[j] - 1, one)
+            pause()
+            one(early[j] - 1)
 
     def join(j, to, k):
         a_wait(to, k)
@@ -397,19 +419,30 @@
                 pb[i, yr] += rb[i - 1, yr]
             last(i).start()
 
-    a_slot(3, after3)
-
     def finish(i):
         last(i).wait_recv()
         emit((pb[i, 0] + ry[i - 3]).T, item_chunk(i) * chunk)
 
-    every(4 - end, 6 - 2 * end, finish)
+    a_slot(3, after3, lambda: every(3, 3 + end, finish))
+    every(4, 6 - 2 * end, finish)
     pw[me] = tot[:, :beams] + tot[:, beams:]
 
-    def p_copy(k):
-        return remote(pw.at[me], pw.at[me], p_s.at[k], p_r.at[k], (me + k) % n)
-
-    every(1, n, lambda k: p_copy(k).start())
+    def p_copy(target):
+        return remote(pw.at[me], pw.at[me], p_s.at[target], p_r.at[me], target)
+
+    def p_far(t):
+        p_copy(dev(chip(3 - t // (SIDE * SIDE)), y + 1 + t // SIDE, core + t)).start()
+
+    others = 3 - end
+    every(0, others * SIDE * SIDE, p_far)
+
+    @pl.when(end == 1)
+    def _():
+        for t in range(SIDE * SIDE):
+            p_copy(dev(chip(0), y + 1 + t // SIDE, core + t)).start()
+
+    for t in range(SIDE * SIDE - 1):
+        p_copy(dev(z, y + 1 + t // SIDE, core + t + t // SIDE)).start()
 
     def last_sent(i):
         last(i).wait_send()
@@ -449,38 +482,32 @@
                 b_back(i, yr).wait_send()
 
     def p_landed(k):
-        p_copy(k).wait_send()
-        other = (me + n - k) % n
-        remote(pw.at[other], pw.at[other], p_s.at[k], p_r.at[k], other).wait_recv()
+        other = (me + k) % n
+        p_copy(other).wait_send()
+        remote(pw.at[other], pw.at[other], p_s.at[other], p_r.at[other], other).wait_recv()
 
     every(1, n, p_landed)
     power[...] = pw[...]
 
 
-def conclude(n, lens, formed, power, beams, decibels, sems):
-    pieces = sems.shape[0]
+def conclude(n, formed, power, bands, beams, decibels, level, sems):
+    pieces = sems.shape[0] - 1
     rows = formed.shape[0] // pieces
     copies = []
     for i in range(pieces):
         span = pl.ds(i * rows, rows)
         copies.append(pltpu.make_async_copy(formed.at[span], beams.at[span], sems.at[i]))
         copies[-1].start()
-    bands = decibels.shape[0]
-    band = lax.broadcasted_iota(jnp.int32, decibels.shape, 0)
-    low = jnp.zeros(decibels.shape, jnp.int32)
-    size = jnp.zeros(decibels.shape, jnp.int32)
-    total = 0
-    for b in range(bands):
-        low = jnp.where(band == b, total, low)
-        size = jnp.where(band == b, lens[b], size)
-        total = total + lens[b]
+    low, size = bands[0], bands[1]
     high = low + size
-    summed = jnp.zeros(decibels.shape, jnp.float32)
+    summed = jnp.zeros(level.shape, jnp.float32)
     for u in range(n):
         inside = jnp.logical_and(low <= u, u < high)
         summed = summed + jnp.where(inside, power[u], 0.0)
     mean = summed / (size.astype(jnp.float32) * formed.shape[0])
-    decibels[...] = (10.0 / math.log(10.0)) * jnp.log(mean + epsilon)
+    level[...] = (10.0 / math.log(10.0)) * jnp.log(mean + epsilon)
+    copies.append(pltpu.make_async_copy(level, decibels, sems.at[pieces]))
+    copies[-1].start()
     for copy in copies:
         copy.wait()
 
@@ -493,15 +520,17 @@
     block = (2 * beams, chunk)
     f32, sem = jnp.float32, pltpu.SemaphoreType.DMA
     raw = (2, local_elems)
-    vmem, hbm, smem = (pl.BlockSpec(memory_space=m) for m in (pltpu.VMEM, pl.ANY, pltpu.SMEM))
-    formed, power = pl.pallas_call(
+    vmem, hbm = (pl.BlockSpec(memory_space=m) for m in (pltpu.VMEM, pl.ANY))
+    band_shape = (band_len.shape[0], beams)
+    formed, power, bands = pl.pallas_call(
         functools.partial(kernel, n),
         out_shape=(
             pltpu.VMEM((unit_cols, 2, beams), f32),
             pltpu.VMEM((n, 1, beams), f32),
+            pltpu.VMEM((2,) + band_shape, jnp.int32),
         ),
         in_specs=[hbm] * 5,
-        out_specs=(vmem, vmem),
+        out_specs=(vmem, vmem, vmem),
         scratch_shapes=[
             pltpu.SMEM(band_len.shape, jnp.int32),
             pltpu.VMEM(delays.shape, f32),
@@ -535,18 +564,17 @@
         band_len, snapshots, delays,
         element_order.reshape(n, 1, local_elems), beam_table.reshape(1, beams),
     )
-    formed = pltpu.with_memory_space_constraint(formed, pltpu.VMEM)
-    power = pltpu.with_memory_space_constraint(power, pltpu.VMEM)
+    parts = [pltpu.with_memory_space_constraint(v, pltpu.VMEM) for v in (formed, power, bands)]
     return pl.pallas_call(
         functools.partial(conclude, n),
         out_shape=(
             jax.ShapeDtypeStruct((unit_cols, 2, beams), f32),
-            jax.ShapeDtypeStruct((band_len.shape[0], beams), f32),
+            jax.ShapeDtypeStruct(band_shape, f32),
         ),
-        in_specs=[smem, vmem, vmem],
-        out_specs=(hbm, vmem),
-        scratch_shapes=[sem((8,))],
-    )(band_len, formed, power)
+        in_specs=[vmem] * 3,
+        out_specs=(hbm, hbm),
+        scratch_shapes=[pltpu.VMEM(band_shape, f32), sem((9,))],
+    )(*parts)
 
 
 def fits(mesh):

time: 175 us -> 173 us (0.989)
  no operation moved by 1% of the time
where the time goes in v3:
time: 173 us
  Pallas kernels  173 us (100%)
    pallas_call x1, Pallas kernels, local_ring(): pl.pallas_call(functools.partial(kernel, n), out_shape=(pltpu.VMEM((unit_...  171 us

profile of v3, /device:TPU:0, one launch (start us, length us, event | category | flops | bytes accessed | tf_op | source)
XLA Modules:
  0.0 173.3 jit_solution(5620186102733190195)
XLA Ops:
  0.6 171.1 %shard_map.68 = (f32[1024,2,256]{2,1,0:T(2,128)S(1)}, f32[16,1,256]{2,1,0:T(1,128)S(1)}, s32[2,8,256]{2,1,0:T(8,128)S(1)}) custom-call(s32[8]{0:T(128)} %lens.1, f32[2,128,16384]{2,1,0:T(8,128)} %x.1, f32[384,2048]{1,0:T(8,128)} %delays.1, s32[16,1,128]{2,1,0:T(1,128)} %bitcast.2, s32[1,256]{1,0:T(1,128)} %bitcast.3), custom_call_target="tpu_custom_call" | custom-call | tf_op jit(solution)/shard_map/pallas_call | solution.py:525
  171.8 1.4 shard_map.69

commit v4 on v3

--- a/solution.py
+++ b/solution.py
@@ -64,7 +64,7 @@
 
 def kernel(
     n, lens, x, delays, order, table, out, power, bands,
-    bl, dl, od, tb, g1, dt, wh, wl, xa, xb, xz, pa, pb, ra, rb, ry, pw, tot,
+    bl, dl, od, tb, g1, dt, wh, wl, xa, xb, xz, pa, pb, ra, rb, ry, fin, tot,
     in_s, own_a, own_b, sa_s, sa_r, sb_s, sb_r, sy_s, sy_r, sz_s, sz_r,
     a_s, a_r, b_s, b_r, y2_s, y2_r, p_s, p_r,
 ):
@@ -176,30 +176,51 @@
 
     pairs = [(yr, r) for yr in (1, 0) for r in (0, 1)]
 
-    def y_start(j):
+    def issue(low):
         def start(k):
             for r in (0, 1):
-                y_copy(j, k, r).start()
-
-        every(0, early[j], start)
+                y_copy(0, k, r).start()
+
+        every(low, early[0], start)
+
+        @pl.when(end == 0)
+        def _():
+            def start(t):
+                for r in (0, 1):
+                    z_copy(t // 2, 1 - t % 2, r).start()
+
+            every(low, 8, start)
+
+        for j in (1, 2, 3):
+            def start(k, j=j):
+                for r in (0, 1):
+                    y_copy(j, k, r).start()
+
+            every(0, early[j], start)
+
+    first = 1
+    for r in (0, 1)[:first]:
+        y_copy(0, 0, r).start()
 
     @pl.when(end == 0)
     def _():
-        for r in (0, 1):
+        for r in (0, 1)[:first]:
             z_copy(0, 1, r).start()
 
-    y_start(0)
-
-    @pl.when(end == 0)
-    def _():
-        def start(t):
-            for r in (0, 1):
-                z_copy(t // 2, 1 - t % 2, r).start()
-
-        every(1, 8, start)
-
-    for j in (1, 2, 3):
-        y_start(j)
+    def rest():
+        for r in (0, 1)[first:]:
+            y_copy(0, 0, r).start()
+
+        @pl.when(end == 0)
+        def _():
+            for r in (0, 1)[first:]:
+                z_copy(0, 1, r).start()
+
+        issue(1)
+
+    @pl.when(core == 0)
+    def _():
+        rest()
 
     ca, la = {}, {}
 
@@ -264,7 +285,13 @@
         got = jnp.dot(g1[...], hot, preferred_element_type=jnp.float32)
         dt[s] = got[:beams] + got[beams:2 * beams] + got[2 * beams:]
 
-    every(0, 6, pick_elems)
+    every(0, 2, pick_elems)
+
+    @pl.when(core == 1)
+    def _():
+        rest()
+
+    every(2, 6, pick_elems)
     wide = 2 * x.shape[1]
 
     def weigh(f, sources):
@@ -341,10 +368,13 @@
         def _():
             join1(k)
 
-    def emit(got, start):
+    def put(got, start):
         rows = pl.ds(pl.multiple_of(start, 128), chunk)
         out[rows, 0, :] = got[:, :beams]
         out[rows, 1, :] = got[:, beams:]
+
+    def emit(got, start):
+        put(got, start)
         tot[...] += jnp.sum(got * got, axis=0, keepdims=True)
 
     def after3(k):
@@ -353,7 +383,10 @@
             join(3, 4, k)
 
         a_wait(2, k)
-        emit((pa[3, k] + ra[2, k]).T, k * chunk)
+
+        @pl.when(k < most - 1)
+        def _():
+            emit((pa[3, k] + ra[2, k]).T, k * chunk)
 
     tot[...] = jnp.zeros_like(tot)
 
@@ -424,11 +457,23 @@
         emit((pb[i, 0] + ry[i - 3]).T, item_chunk(i) * chunk)
 
     a_slot(3, after3, lambda: every(3, 3 + end, finish))
-    every(4, 6 - 2 * end, finish)
-    pw[me] = tot[:, :beams] + tot[:, beams:]
+
+    @pl.when(end == 0)
+    def _():
+        finish(4)
+        last(5).wait_recv()
+        fin[...] = pb[5, 0] + ry[2]
+
+    @pl.when(end == 1)
+    def _():
+        fin[...] = pa[3, most - 1] + ra[2, most - 1]
+
+    squares = fin[...] * fin[...]
+    late_row = jnp.sum((squares[:beams] + squares[beams:]).T, axis=0, keepdims=True)
+    power[me] = tot[:, :beams] + tot[:, beams:] + late_row
 
     def p_copy(target):
-        return remote(pw.at[me], pw.at[me], p_s.at[target], p_r.at[me], target)
+        return remote(power.at[me], power.at[me], p_s, p_r, target)
 
     def p_far(t):
         p_copy(dev(chip(3 - t // (SIDE * SIDE)), y + 1 + t // SIDE, core + t)).start()
@@ -443,6 +488,8 @@
 
     for t in range(SIDE * SIDE - 1):
         p_copy(dev(z, y + 1 + t // SIDE, core + t + t // SIDE)).start()
+
+    put(fin[...].T, (most - 1) * chunk)
 
     def last_sent(i):
         last(i).wait_send()
@@ -481,13 +528,8 @@
             for i in (4, 5):
                 b_back(i, yr).wait_send()
 
-    def p_landed(k):
-        other = (me + k) % n
-        p_copy(other).wait_send()
-        remote(pw.at[other], pw.at[other], p_s.at[other], p_r.at[other], other).wait_recv()
-
-    every(1, n, p_landed)
-    power[...] = pw[...]
+    rest = power.at[pl.ds(0, n - 1)]
+    remote(rest, rest, p_s, p_r, beside).wait()
 
 
 def conclude(n, formed, power, bands, beams, decibels, level, sems):
@@ -548,14 +590,14 @@
             pltpu.VMEM((5, most) + block, f32),
             pltpu.VMEM((5, 2) + block, f32),
             pltpu.VMEM((3,) + block, f32),
-            pltpu.VMEM((n, 1, beams), f32),
+            pltpu.VMEM(block, f32),
             pltpu.VMEM((1, 2 * beams), f32),
             sem((4,)), sem((4,)), sem((6, 2)),
             sem((4,)), sem((4,)), sem((6, 2)), sem((6, 2)),
             sem((2, 4, most)), sem((2, 4, most)), sem((4, 2, 2)), sem((4, 2, 2)),
             sem((3, most)), sem((5, most)), sem((5, 2)), sem((5, 2)),
             sem((3,)), sem((3,)),
-            sem((n,)), sem((n,)),
+            sem, sem,
         ],
         compiler_params=pltpu.CompilerParams(
             collective_id=0, has_side_effects=True, vmem_limit_bytes=54 * 1024 * 1024

time: 173 us -> 173 us (level)
  no operation moved by 1% of the time
where the time goes in v4:
time: 173 us; the launch traced here: 172 us
  Pallas kernels  172 us (99%)
    pallas_call x1, Pallas kernels, local_ring(): pl.pallas_call(functools.partial(kernel, n), out_shape=(pltpu.VMEM((unit_...  170 us

profile of v4, /device:TPU:0, one launch (start us, length us, event | category | flops | bytes accessed | tf_op | source)
XLA Modules:
  0.0 172.5 jit_solution(16228577364249204056)
XLA Ops:
  0.6 170.3 %shard_map.68 = (f32[1024,2,256]{2,1,0:T(2,128)S(1)}, f32[16,1,256]{2,1,0:T(1,128)S(1)}, s32[2,8,256]{2,1,0:T(8,128)S(1)}) custom-call(s32[8]{0:T(128)} %lens.1, f32[2,128,16384]{2,1,0:T(8,128)} %x.1, f32[384,2048]{1,0:T(8,128)} %delays.1, s32[16,1,128]{2,1,0:T(1,128)} %bitcast.2, s32[1,256]{1,0:T(1,128)} %bitcast.3), custom_call_target="tpu_custom_call" | custom-call | tf_op jit(solution)/shard_map/pallas_call | solution.py:567
  170.9 1.4 shard_map.69

commit v5 on v4

--- a/solution.py
+++ b/solution.py
@@ -176,12 +176,12 @@
 
     pairs = [(yr, r) for yr in (1, 0) for r in (0, 1)]
 
-    def issue(low):
+    def issue():
         def start(k):
             for r in (0, 1):
                 y_copy(0, k, r).start()
 
-        every(low, early[0], start)
+        every(1, early[0], start)
 
         @pl.when(end == 0)
         def _():
@@ -189,7 +189,7 @@
                 for r in (0, 1):
                     z_copy(t // 2, 1 - t % 2, r).start()
 
-            every(low, 8, start)
+            every(1, 8, start)
 
         for j in (1, 2, 3):
             def start(k, j=j):
@@ -198,25 +198,20 @@
 
             every(0, early[j], start)
 
-    first = 1
-    for r in (0, 1)[:first]:
-        y_copy(0, 0, r).start()
+    y_copy(0, 0, 0).start()
 
     @pl.when(end == 0)
     def _():
-        for r in (0, 1)[:first]:
-            z_copy(0, 1, r).start()
+        z_copy(0, 1, 0).start()
 
     def rest():
-        for r in (0, 1)[first:]:
-            y_copy(0, 0, r).start()
+        y_copy(0, 0, 1).start()
 
         @pl.when(end == 0)
         def _():
-            for r in (0, 1)[first:]:
-                z_copy(0, 1, r).start()
-
-        issue(1)
+            z_copy(0, 1, 1).start()
+
+        issue()
 
     @pl.when(core == 0)
     def _():
@@ -285,13 +280,13 @@
         got = jnp.dot(g1[...], hot, preferred_element_type=jnp.float32)
         dt[s] = got[:beams] + got[beams:2 * beams] + got[2 * beams:]
 
-    every(0, 2, pick_elems)
+    every(0, 1, pick_elems)
 
     @pl.when(core == 1)
     def _():
         rest()
 
-    every(2, 6, pick_elems)
+    every(1, 6, pick_elems)
     wide = 2 * x.shape[1]
 
     def weigh(f, sources):

time: 173 us -> 172 us (level)
  no operation moved by 1% of the time
where the time goes in v5:
time: 172 us
  Pallas kernels  171 us (99%)
    pallas_call x1, Pallas kernels, local_ring(): pl.pallas_call(functools.partial(kernel, n), out_shape=(pltpu.VMEM((unit_...  170 us

profile of v5, /device:TPU:0, one launch (start us, length us, event | category | flops | bytes accessed | tf_op | source)
XLA Modules:
  0.0 172.2 jit_solution(14902162327341194035)
XLA Ops:
  0.6 170.0 %shard_map.68 = (f32[1024,2,256]{2,1,0:T(2,128)S(1)}, f32[16,1,256]{2,1,0:T(1,128)S(1)}, s32[2,8,256]{2,1,0:T(8,128)S(1)}) custom-call(s32[8]{0:T(128)} %lens.1, f32[2,128,16384]{2,1,0:T(8,128)} %x.1, f32[384,2048]{1,0:T(8,128)} %delays.1, s32[16,1,128]{2,1,0:T(1,128)} %bitcast.2, s32[1,256]{1,0:T(1,128)} %bitcast.3), custom_call_target="tpu_custom_call" | custom-call | tf_op jit(solution)/shard_map/pallas_call | solution.py:562
  170.7 1.4 shard_map.69

commit v6 on v5

--- a/solution.py
+++ b/solution.py
@@ -66,7 +66,7 @@
     n, lens, x, delays, order, table, out, power, bands,
     bl, dl, od, tb, g1, dt, wh, wl, xa, xb, xz, pa, pb, ra, rb, ry, fin, tot,
     in_s, own_a, own_b, sa_s, sa_r, sb_s, sb_r, sy_s, sy_r, sz_s, sz_r,
-    a_s, a_r, b_s, b_r, y2_s, y2_r, p_s, p_r,
+    a_s, a_r, b_s, b_r, y2_s, y2_r, f_s, f_r, p_s, p_r,
 ):
     me = lax.axis_index("elem")
     core = me % SIDE
@@ -167,6 +167,19 @@
         return remote(pb.at[i, 1], ry.at[i - 3], y2_s.at[i - 3], y2_r.at[i - 3],
                       dev(z, y + 1, core))
 
+    half = beams // 2
+
+    def quarter(b):
+        return pl.ds(b * half, half)
+
+    def y_final(b):
+        return remote(pb.at[5, 1, quarter(b)], ry.at[2, quarter(b)],
+                      f_s.at[0, b], f_r.at[0, b], dev(z, y + 1, core))
+
+    def z_final(b):
+        return remote(pa.at[2, most - 1, quarter(b)], ra.at[2, most - 1, quarter(b)],
+                      f_s.at[1, b], f_r.at[1, b], beside)
+
     def every(low, high, step):
         def body(t, carry):
             step(t)
@@ -357,7 +370,14 @@
         def _():
             join(2, 3, k)
 
-        a_copy(2, k).start()
+        @pl.when(k < most - 1)
+        def _():
+            a_copy(2, k).start()
+
+        @pl.when(k == most - 1)
+        def _():
+            for b in (0, 2, 1, 3):
+                z_final(b).start()
 
         @pl.when(end == 1)
         def _():
@@ -377,10 +397,9 @@
         def _():
             join(3, 4, k)
 
-        a_wait(2, k)
-
         @pl.when(k < most - 1)
         def _():
+            a_wait(2, k)
             emit((pa[3, k] + ra[2, k]).T, k * chunk)
 
     tot[...] = jnp.zeros_like(tot)
@@ -445,7 +464,9 @@
             for yr in (1, 0):
                 b_back(i, yr).wait_recv()
                 pb[i, yr] += rb[i - 1, yr]
-            last(i).start()
+        last(4).start()
+        for b in (0, 2, 1, 3):
+            y_final(b).start()
 
     def finish(i):
         last(i).wait_recv()
@@ -456,16 +477,24 @@
     @pl.when(end == 0)
     def _():
         finish(4)
-        last(5).wait_recv()
-        fin[...] = pb[5, 0] + ry[2]
-
-    @pl.when(end == 1)
-    def _():
-        fin[...] = pa[3, most - 1] + ra[2, most - 1]
-
-    squares = fin[...] * fin[...]
-    late_row = jnp.sum((squares[:beams] + squares[beams:]).T, axis=0, keepdims=True)
-    power[me] = tot[:, :beams] + tot[:, beams:] + late_row
+
+    early_power = tot[:, :beams] + tot[:, beams:]
+    for p in (0, 1):
+        @pl.when(end == 0)
+        def _():
+            for b in (p, p + 2):
+                y_final(b).wait_recv()
+                fin[quarter(b)] = pb[5, 0, quarter(b)] + ry[2, quarter(b)]
+
+        @pl.when(end == 1)
+        def _():
+            for b in (p, p + 2):
+                z_final(b).wait_recv()
+                fin[quarter(b)] = pa[3, most - 1, quarter(b)] + ra[2, most - 1, quarter(b)]
+
+        real, imag = fin[quarter(p)], fin[quarter(p + 2)]
+        late_row = jnp.sum((real * real + imag * imag).T, axis=0, keepdims=True)
+        power[me, :, quarter(p)] = early_power[:, p * half:(p + 1) * half] + late_row
 
     def p_copy(target):
         return remote(power.at[me], power.at[me], p_s, p_r, target)
@@ -489,7 +518,13 @@
     def last_sent(i):
         last(i).wait_send()
 
-    every(4 - end, 6 - 2 * end, last_sent)
+    every(4 - end, 5 - end, last_sent)
+
+    @pl.when(end == 0)
+    def _():
+        for b in range(4):
+            y_final(b).wait_send()
+            z_final(b).wait_send()
 
     def b_sent(i):
         for yr in (1, 0):
@@ -502,10 +537,12 @@
         def drain(k, j=j):
             for r in (0, 1):
                 y_copy(j, k, r).wait_send()
-            if j < 3:
+            if j < 2:
                 a_copy(j, k).wait_send()
 
         every(0, early[j], drain)
+
+    every(0, most - 1, lambda k: a_copy(2, k).wait_send())
 
     @pl.when(end == 0)
     def _():
@@ -592,6 +629,7 @@
             sem((2, 4, most)), sem((2, 4, most)), sem((4, 2, 2)), sem((4, 2, 2)),
             sem((3, most)), sem((5, most)), sem((5, 2)), sem((5, 2)),
             sem((3,)), sem((3,)),
+            sem((2, 4)), sem((2, 4)),
             sem, sem,
         ],
         compiler_params=pltpu.CompilerParams(

time: 172 us -> 172 us (level)
  no operation moved by 1% of the time
where the time goes in v6:
time: 172 us
  Pallas kernels  172 us (100%)
    pallas_call x1, Pallas kernels, local_ring(): pl.pallas_call(functools.partial(kernel, n), out_shape=(pltpu.VMEM((unit_...  170 us

profile of v6, /device:TPU:0, one launch (start us, length us, event | category | flops | bytes accessed | tf_op | source)
XLA Modules:
  0.0 172.3 jit_solution(2507775586319268221)
XLA Ops:
  0.6 170.2 %shard_map.68 = (f32[1024,2,256]{2,1,0:T(2,128)S(1)}, f32[16,1,256]{2,1,0:T(1,128)S(1)}, s32[2,8,256]{2,1,0:T(8,128)S(1)}) custom-call(s32[8]{0:T(128)} %lens.1, f32[2,128,16384]{2,1,0:T(8,128)} %x.1, f32[384,2048]{1,0:T(8,128)} %delays.1, s32[16,1,128]{2,1,0:T(1,128)} %bitcast.2, s32[1,256]{1,0:T(1,128)} %bitcast.3), custom_call_target="tpu_custom_call" | custom-call | tf_op jit(solution)/shard_map/pallas_call | solution.py:599
  170.8 1.4 shard_map.69

commit v7 on v6

--- a/solution.py
+++ b/solution.py
@@ -97,8 +97,9 @@
         pl.semaphore_signal(barrier, inc=1, device_id={"elem": target},
                             device_id_type=pl.DeviceIdType.MESH)
 
-    for r in (0, 1):
+    for r in (1, 0):
         greet(dev(z, y + 1, core + r))
+    for r in (1, 0):
         greet(dev(chip(1 - end), y, core + r))
     greet(dev(z, y, core + 1))
 

time: 172 us -> 172 us (level)
  no operation moved by 1% of the time
where the time goes in v7:
time: 172 us
  Pallas kernels  172 us (100%)
    pallas_call x1, Pallas kernels, local_ring(): pl.pallas_call(functools.partial(kernel, n), out_shape=(pltpu.VMEM((unit_...  170 us

profile of v7, /device:TPU:0, one launch (start us, length us, event | category | flops | bytes accessed | tf_op | source)
XLA Modules:
  0.0 172.3 jit_solution(13736659446009824918)
XLA Ops:
  0.6 170.1 %shard_map.68 = (f32[1024,2,256]{2,1,0:T(2,128)S(1)}, f32[16,1,256]{2,1,0:T(1,128)S(1)}, s32[2,8,256]{2,1,0:T(8,128)S(1)}) custom-call(s32[8]{0:T(128)} %lens.1, f32[2,128,16384]{2,1,0:T(8,128)} %x.1, f32[384,2048]{1,0:T(8,128)} %delays.1, s32[16,1,128]{2,1,0:T(1,128)} %bitcast.2, s32[1,256]{1,0:T(1,128)} %bitcast.3), custom_call_target="tpu_custom_call" | custom-call | tf_op jit(solution)/shard_map/pallas_call | solution.py:600
  170.8 1.4 shard_map.69
